TPU v7x, 128 devices: a 2x2x16 block of a 8x8x16 slice. The times are simulated.
128 devices in a mesh: mol: 4 (over y, x), pts: 32 (over z, core).
Axes of the slice: x: 2, y: 2, z: 16, core: 2. Of those that a mesh axis runs over, the one named last changes fastest.
The devices are a block of a 8x8x16 slice.
Arguments:
- points_map: bfloat16 [25600, 800], P(('mol', 'pts')), parts along dimension 0, may hold values from -0.21875 to 0.21875
- trial: bfloat16 [25600, 128], P('mol'), parts along dimension 0, may hold values from -6 to 6
- core: bfloat16 [25600, 6400], P(('mol', 'pts')), parts along dimension 0, may hold values from -2 to 4, as said below
- walkers: bfloat16 [3200, 12, 128], P('mol'), parts along dimension 0, may hold values from -6 to 6
- draws: int32 [25600, 12], P(('mol', 'pts')), parts along dimension 0, may hold values from 0 to 3
Outputs:
- new_walkers: bfloat16 [3200, 12, 128], P(('mol', 'pts')), parts along dimension 0
- energy: float32 [48], P('mol'), parts along dimension 0
There are 4 independent parts, one for each index of `mol`. A program takes and returns all parts, laid end to end along the dimension named above; each array names one. Nothing has to cross between parts.
Inputs may be any that keep to these rules, and one draw needn't show every extreme that they name: core is symmetric.
All inputs are finite; a program needn't handle non-finite values.
Results may differ from a plain program's by a relative error of at most 0.018.
Values may be sent and summed in bfloat16 or wider, within the bound.
No kernel may reach another device: no remote copies, remote signals or barrier semaphores. Data moves between devices by JAX's collectives and lax.ppermute only.
A program may use at most 192 MiB of HBM per device.

v0:
```python
import math
import jax
import jax.numpy as jnp
from jax import lax
from jax.sharding import PartitionSpec as P

TAYLOR = 3
GAUSS_NODES = (-2.3344142, -0.7419637, 0.7419637, 2.3344142)
FIELD_STEP = 0.15


def copy_for_each(value, axis):
    copies = jnp.broadcast_to(value, (lax.axis_size(axis), *value.shape))
    return lax.all_to_all(copies, axis, split_axis=0, concat_axis=0, tiled=True)


def joined_along(pieces, dim):
    lengths = list(pieces.shape[1:])
    lengths[dim] *= pieces.shape[0]
    return jnp.moveaxis(pieces, 0, dim).reshape(lengths)


def gathered_copies(value, axis, dim):
    pieces = copy_for_each(value, axis)
    return joined_along(pieces, dim)


def over_copies(value, axis):
    everything = copy_for_each(value, axis)
    return jnp.sum(everything, axis=0)


def node_lookup(draws):
    values = jnp.zeros(draws.shape, jnp.float32)
    for number, node in enumerate(GAUSS_NODES):
        values = values + jnp.where(draws == number, node, 0.0).astype(jnp.float32)
    return values


def body(points_map, trial, core, walkers, draws):
    point_rows = points_map.shape[0]
    orbitals = points_map.shape[1]
    walker_count = walkers.shape[1]
    occupied = walkers.shape[2]
    point_first = lax.axis_index("pts") * point_rows
    trial_here = lax.dynamic_slice_in_dim(trial, point_first, point_rows, 0)
    flat_walkers = walkers.reshape(orbitals, walker_count * occupied)
    orbit = (
        jnp.dot(points_map, flat_walkers, preferred_element_type=jnp.float32)
        .astype(jnp.bfloat16)
        .reshape(point_rows, walker_count, occupied)
    )
    density = (
        jnp.sum(orbit.astype(jnp.float32) * trial_here.astype(jnp.float32)[:, None, :], axis=2)
        / math.sqrt(occupied)
    ).astype(jnp.bfloat16)
    core_block = core
    potential = jnp.dot(
        core_block, gathered_copies(density, "pts", 0), preferred_element_type=jnp.float32
    )
    field = FIELD_STEP * (node_lookup(draws) - FIELD_STEP * potential)
    local_walkers = jnp.moveaxis(orbit, 1, 0)
    shard_piece = lax.all_gather(points_map, "pts", axis=0, tiled=True)
    remote = (
        jnp.dot(shard_piece, flat_walkers, preferred_element_type=jnp.float32)
        .astype(jnp.bfloat16)
        .reshape(shard_piece.shape[0], walker_count, occupied)
    )
    core_block = core.astype(jnp.float32)

    def per_walker(operands):
        left_orb, right_orb = operands
        forward = jnp.dot(left_orb, trial.T, preferred_element_type=jnp.float32)
        backward = jnp.dot(trial_here, right_orb.T, preferred_element_type=jnp.float32)
        return jnp.sum(core_block * forward * backward)

    exchange = lax.map(per_walker, (local_walkers, jnp.moveaxis(remote, 1, 0))) / occupied
    hartree = jnp.sum(density.astype(jnp.float32) * potential, axis=0)
    total_points = point_rows * lax.axis_size("pts")
    energy = over_copies((hartree - exchange) / (2.0 * total_points), "pts")
    own_rows = orbitals // lax.axis_size("pts")
    map_full = lax.all_gather(points_map, "pts", axis=0, tiled=True)
    field_full = gathered_copies(field, "pts", 0)
    own_cols = walker_count * occupied // lax.axis_size("pts")
    col_start = lax.axis_index("pts") * own_cols
    cols_walkers = lax.dynamic_slice_in_dim(flat_walkers, col_start, own_cols, 1)
    walker_ids = (col_start + jnp.arange(own_cols, dtype=jnp.int32)) // occupied
    field_cols = jnp.take(field_full, walker_ids, axis=1)
    running_cols = cols_walkers.astype(jnp.float32)
    term_cols = cols_walkers
    for degree in range(1, TAYLOR + 1):
        current_cols = jnp.dot(map_full, term_cols, preferred_element_type=jnp.float32).astype(
            jnp.bfloat16
        )
        scaled_cols = (field_cols * current_cols.astype(jnp.float32)).astype(jnp.bfloat16)
        summed_cols = jnp.einsum(
            "pi,pc->ic", map_full, scaled_cols, preferred_element_type=jnp.float32
        )
        term_cols = (summed_cols / degree).astype(jnp.bfloat16)
        running_cols = running_cols + term_cols.astype(jnp.float32)
    placed = lax.all_to_all(
        running_cols.astype(jnp.bfloat16), "pts", split_axis=0, concat_axis=1, tiled=True
    )
    return (placed.reshape(own_rows, walker_count, occupied), energy)


def solution(mesh):
    placed = (
        P(("mol", "pts"), None),
        P("mol", None),
        P(("mol", "pts"), None),
        P("mol", None, None),
        P(("mol", "pts"), None),
    )
    return jax.shard_map(
        body,
        mesh=mesh,
        in_specs=placed,
        out_specs=(P(("mol", "pts"), None, None), P("mol")),
        check_vma=False,
    )
```

profile of v0, /device:TPU:70, one launch (start us, length us, event | category | flops | bytes accessed | tf_op | source)
XLA Modules:
  0.0 349.0 jit_solution(5350496346310560887)
XLA Ops:
  8.0 4.4 %copy.54 = bf16[800,12,128]{0,2,1:T(8,128)(2,1)} copy(bf16[800,12,128]{2,0,1:T(8,128)(2,1)} %param.10) | data formatting | bytes 4915200 | tf_op args[3]
  16.5 42.7 %all_to_all.32 = bf16[32,200,12]{1,2,0:T(8,128)(2,1)S(1)} all-to-all(bf16[32,200,12]{1,2,0:T(8,128)(2,1)S(1)} %broadcast_in_dim.50), channel_id=1, replica_groups=mesh['mol'=4,'pts'=32] {'pts'}, dimensions={0} | all-to-all | bytes 307200 | tf_op jit(solution)/shard_map/all_to_all | solution.py:14
  63.2 5.0 %all-to-all-start.1 = ((f32[32,200,12]{1,2,0:T(8,128)}), f32[32,200,12]{1,2,0:T(8,128)S(1)}, u32[]{:S(2)}, u32[]{:S(2)}) async-start(f32[32,200,12]{1,2,0:T(8,128)} %broadcast_in_dim.51), calls=%async_computation.1 | async-start | bytes 1048576 | tf_op jit(solution)/shard_map/all_to_all | solution.py:14
  68.2 4.4 %convert_element_type.124 = f32[200,6400]{1,0:T(8,128)} convert(bf16[200,6400]{1,0:T(8,128)(2,1)} %param.9) | non-fusion elementwise | flops 1280000 | bytes 7680000 | tf_op jit(solution)/shard_map/convert_element_type | solution.py:69
  73.7 33.3 %all-to-all-done.1 = f32[32,200,12]{1,2,0:T(8,128)S(1)} async-done(((f32[32,200,12]{1,2,0:T(8,128)}), f32[32,200,12]{1,2,0:T(8,128)S(1)}, u32[]{:S(2)}, u32[]{:S(2)}) %all-to-all-start.1) | async-done | bytes 307232 | tf_op jit(solution)/shard_map/all_to_all | solution.py:14
  108.5 20.6 %all-gather.2.cloned.1.call-done = bf16[6400,800]{1,0:T(8,128)(2,1)} async-done(((bf16[200,800]{1,0:T(8,128)(2,1)}), bf16[6400,800]{1,0:T(8,128)(2,1)}) %all-gather.2.cloned.1.call-update) | async-done | bytes 10240016 | tf_op jit(solution)/shard_map/all_gather | solution.py:82
  129.1 28.2 %convolution_convert_fusion = bf16[6400,1536]{0,1:T(8,128)(2,1)} fusion(bf16[6400,800]{1,0:T(8,128)(2,1)} %all-gather.2.cloned.1.call-done, bf16[800,1536]{0,1:T(8,128)(2,1)} %bitcast.69), kind=kOutput, calls=%fused_computation.11 | convolution fusion | flops 15738470400 | bytes 32358400 | tf_op jit(solution)/shard_map/dot_general | solution.py:65
  157.4 26.2 %copy.60 = bf16[6400,12,128]{2,0,1:T(8,128)(2,1)} copy(bf16[6400,12,128]{0,2,1:T(8,128)(2,1)} %bitcast.67) | data formatting | bytes 39321600 | tf_op jit(solution)/shard_map/reshape | solution.py:67
  183.5 81.9 %while.10 = (s32[]{:T(128)}, f32[12]{0:T(128)S(1)}, bf16[12,200,128]{2,1,0:T(8,128)(2,1)}, bf16[6400,128]{1,0:T(8,128)(2,1)S(1)}, f32[200,6400]{1,0:T(8,128)}, /...) while((s32[]{:T(128)}, f32[12]{0:T(128)S(1)}, bf16[12,200,128]{2,1,0:T(8,128)(2,1)}, ...), condition=%wide.region_4.5_spmd, body=%wide.region_2.4_spmd.sunk | while | flops 659200000 | bytes 34100372 | solution.py:77
  186.5 3.1 fusion.63
  193.3 3.1 fusion.63
  200.1 3.1 fusion.63
  206.9 3.1 fusion.63
  213.7 3.1 fusion.63
  220.6 3.1 fusion.63
  227.4 3.1 fusion.63
  234.2 3.1 fusion.63
  254.7 3.1 fusion.63
  266.0 9.1 %all-to-all-start.3 = ((f32[32,1,12]{2,1,0:T(1,128)}), f32[32,1,12]{2,1,0:T(1,128)S(1)}, u32[]{:S(2)}, u32[]{:S(2)}) async-start(f32[32,1,12]{2,1,0:T(1,128)} %broadcast_in_dim.53), calls=%async_computation.3 | async-start | bytes 32768 | tf_op jit(solution)/shard_map/all_to_all | solution.py:14
  275.1 12.6 %convolution_convert_fusion.5 = bf16[48,800]{1,0:T(8,128)(2,1)S(1)} fusion(bf16[6400,800]{1,0:T(8,128)(2,1)} %all-gather.2.cloned.1.call-done, f32[48,6400]{1,0:T(8,128)S(1)} %gather_fusion, pred[48]{0:T(512)(128)(4,1)S(1)} %compare_and_fusion, bf16[800,1536]{0,1:T(8,128)(2,1)} %bitcast.70, s32[]{:T(128)S(6)} %select_n.54), kind=kOutput, calls=%fused_computation.34 | convolution fusion | flops 984614400 | bytes 24329268 | tf_op jit(solution)/shard_map/pi,pc->ic/dot_general | solution.py:96
  287.7 12.6 %fusion.17 = bf16[48,800]{1,0:T(8,128)(2,1)S(1)} fusion(bf16[6400,800]{1,0:T(8,128)(2,1)} %all-gather.2.cloned.1.call-done, bf16[48,800]{1,0:T(8,128)(2,1)S(1)} %convolution_convert_fusion.5, f32[48,6400]{1,0:T(8,128)S(1)} %gather_fusion, pred[48]{0:T(512)(128)(4,1)S(1)} %compare_and_fusion), kind=kOutput, calls=%fused_computation.28 | convolution fusion | flops 984652800 | bytes 11622448 | tf_op jit(solution)/shard_map/pi,pc->ic/dot_general | solution.py:96
  300.3 12.6 %fusion.22 = bf16[800,48]{0,1:T(8,128)(2,1)S(1)} fusion(bf16[6400,800]{1,0:T(8,128)(2,1)} %all-gather.2.cloned.1.call-done, bf16[48,800]{1,0:T(8,128)(2,1)S(1)} %fusion.17, f32[48,6400]{1,0:T(8,128)S(1)} %gather_fusion, pred[48]{0:T(512)(128)(4,1)S(1)} %compare_and_fusion, bf16[48,800]{1,0:T(8,128)(2,1)S(1)} %convolution_convert_fusion.5, ...), kind=kOutput, calls=%fused_computation.33 | convolution fusion | flops 984960000 | bytes 24587780 | tf_op jit(solution)/shard_map/pi,pc->ic/dot_general | solution.py:96
  314.1 12.2 %all-to-all-start.2 = ((bf16[32,2,600]{2,1,0:T(2,128)(2,1)}), bf16[32,2,600]{2,1,0:T(2,128)(2,1)S(1)}, u32[]{:S(2)}, u32[]{:S(2)}) async-start(bf16[32,2,600]{2,1,0:T(2,128)(2,1)} %reshape.111), calls=%async_computation.2 | async-start | bytes 163840 | tf_op jit(solution)/shard_map/all_to_all | solution.py:101
  326.9 13.8 %all-to-all-done.2 = bf16[32,2,600]{2,1,0:T(2,128)(2,1)S(1)} async-done(((bf16[32,2,600]{2,1,0:T(2,128)(2,1)}), bf16[32,2,600]{2,1,0:T(2,128)(2,1)S(1)}, u32[]{:S(2)}, u32[]{:S(2)}) %all-to-all-start.2) | async-done | bytes 76832 | tf_op jit(solution)/shard_map/all_to_all | solution.py:101
  (125 shorter events, 68.7 us)
Async XLA Ops:
  7.2 5.3 %copy-start.1 = (bf16[200,800]{1,0:T(8,128)(2,1)S(1)}, bf16[200,800]{1,0:T(8,128)(2,1)}, u32[]{:S(2)}) copy-start(bf16[200,800]{1,0:T(8,128)(2,1)} %param.7) | copy-start | bytes 960004
  7.2 121.9 %all-gather.2.cloned.1.call-start = ((), (), s32[]{:S(2)}) async-start(), calls=%async_computation.4 | async-start | bytes 11827200 | tf_op jit(solution)/shard_map/all_gather | solution.py:82
  12.4 3.4 copy-start
  15.4 44.2 %copy-start.2 = (s32[200,12]{0,1:T(8,128)S(1)}, s32[200,12]{0,1:T(8,128)}, u32[]{:S(2)}) copy-start(s32[200,12]{0,1:T(8,128)} %param.11) | copy-start | bytes 28804
  63.2 43.8 %all-to-all-start.1 = ((f32[32,200,12]{1,2,0:T(8,128)}), f32[32,200,12]{1,2,0:T(8,128)S(1)}, u32[]{:S(2)}, u32[]{:S(2)}) async-start(f32[32,200,12]{1,2,0:T(8,128)} %broadcast_in_dim.51), calls=%async_computation.1 | async-start | bytes 1048576 | tf_op jit(solution)/shard_map/all_to_all | solution.py:14
  183.5 2.9 slice-start.1
  190.3 2.8 slice-start
  190.3 2.9 slice-start.1
  197.2 2.8 slice-start
  197.2 2.9 slice-start.1
  204.0 2.8 slice-start
  204.0 2.9 slice-start.1
  210.8 2.8 slice-start
  210.8 2.9 slice-start.1
  217.6 2.8 slice-start
  217.6 2.9 slice-start.1
  224.4 2.9 slice-start.1
  231.3 2.9 slice-start.1
  238.1 2.9 slice-start.1
  244.9 2.9 slice-start.1
  251.7 2.9 slice-start.1
  258.6 2.9 slice-start.1
  266.0 48.1 %all-to-all-start.3 = ((f32[32,1,12]{2,1,0:T(1,128)}), f32[32,1,12]{2,1,0:T(1,128)S(1)}, u32[]{:S(2)}, u32[]{:S(2)}) async-start(f32[32,1,12]{2,1,0:T(1,128)} %broadcast_in_dim.53), calls=%async_computation.3 | async-start | bytes 32768 | tf_op jit(solution)/shard_map/all_to_all | solution.py:14
  314.1 26.6 %all-to-all-start.2 = ((bf16[32,2,600]{2,1,0:T(2,128)(2,1)}), bf16[32,2,600]{2,1,0:T(2,128)(2,1)S(1)}, u32[]{:S(2)}, u32[]{:S(2)}) async-start(bf16[32,2,600]{2,1,0:T(2,128)(2,1)} %reshape.111), calls=%async_computation.2 | async-start | bytes 163840 | tf_op jit(solution)/shard_map/all_to_all | solution.py:101
  (7 other events, 19.7 us)
Sparse Core Ops, SparseCore 0:
  9.7 119.3 all-gather.1
where the time goes:
time: 351 us; the launch traced here: 349 us
  matrix products  143 us (41%)
  waiting for transfers between devices  68.5 us (20%)
  local copies, waits for them, and re-layouts  48.7 us (14%)
  blocking collectives  42.7 us (12%)
  starting transfers between devices  26.4 us (8%)
  between operations  14.2 us (4%)
  other arithmetic  5.57 us (2%)
    all_to_all x1, blocking collectives, copy_for_each(): return lax.all_to_all(copies, axis, split_axis=0, concat_axis=0, tiled=True)  42.7 us
    dot_general x3, matrix products, body(): jnp.einsum('pi,pc->ic', map_full, scaled_cols, preferred_element_type=jnp...  37.8 us
    dot_general x12, matrix products, per_walker(): forward = jnp.dot(left_orb, trial.T, preferred_element_type=jnp.float32)  37.5 us
    dot_general x12, matrix products, per_walker(): jnp.dot(trial_here, right_orb.T, preferred_element_type=jnp.float32)  33.6 us
    all_to_all x2, waiting for transfers between devices, copy_for_each(): return lax.all_to_all(copies, axis, split_axis=0, concat_axis=0, tiled=True)  33.3 us
    dot_general x1, matrix products, body(): jnp.dot(shard_piece, flat_walkers, preferred_element_type=jnp.float32)  28.2 us
    reshape x1, local copies, waits for them, and re-layouts, body(): remote = jnp.dot(shard_piece, flat_walkers, preferred_element_type=jnp.fl...  26.2 us
    all_gather x1, waiting for transfers between devices, body(): map_full = lax.all_gather(points_map, 'pts', axis=0, tiled=True)  20.6 us
  transfers between devices with their start and end apart: 4, of which 3 were waited for; matrix products, arithmetic and copies ran while one was open for 17% of the time, Pallas kernels for 0%

commit v1 on v0

--- a/solution.py
+++ b/solution.py
@@ -79,7 +79,8 @@
     total_points = point_rows * lax.axis_size("pts")
     energy = over_copies((hartree - exchange) / (2.0 * total_points), "pts")
     own_rows = orbitals // lax.axis_size("pts")
-    map_full = lax.all_gather(points_map, "pts", axis=0, tiled=True)
+    copies_2 = jnp.concatenate([points_map] * lax.axis_size("pts"), axis=0)
+    map_full = lax.all_to_all(copies_2, "pts", 0, 0, tiled=True)
     field_full = gathered_copies(field, "pts", 0)
     own_cols = walker_count * occupied // lax.axis_size("pts")
     col_start = lax.axis_index("pts") * own_cols

time: 351 us -> 752 us (2.14)
  waiting for transfers between devices: 68.5 us -> 461 us
  blocking collectives: 42.7 us -> 0 us
  local copies, waits for them, and re-layouts: 48.7 us -> 76.8 us
  starting transfers between devices: 26.4 us -> 48.7 us
    all_gather x1, waiting for transfers between devices: 20.6 us -> 330 us  [body(): shard_piece = lax.all_gather(points_map, 'pts', axis=0, tiled=True)]
    all_to_all x0 -> x1, waiting for transfers between devices: none -> 86.7 us  [body(): map_full = lax.all_to_all(copies_2, 'pts', 0, 0, tiled=True)]
    all_to_all x1 -> x0, blocking collectives: 42.7 us -> none  [copy_for_each(): return lax.all_to_all(copies, axis, split_axis=0, concat_axis=0, tiled=True)]
    unnamed x10 -> x49, local copies, waits for them, and re-layouts: 6.53 us -> 30.1 us
    all_to_all x2 -> x3, starting transfers between devices: 14.1 us -> 30.2 us  [copy_for_each(): return lax.all_to_all(copies, axis, split_axis=0, concat_axis=0, tiled=True)]
    all_to_all x2 -> x3, waiting for transfers between devices: 33.3 us -> 30.4 us  [copy_for_each(): return lax.all_to_all(copies, axis, split_axis=0, concat_axis=0, tiled=True)]
  transfers between devices with their start and end apart: 4 -> 6, of which waited for: 3 -> 5; matrix products, arithmetic and copies ran while one was open for 17% -> 27% of each run, Pallas kernels for 0% -> 0%
where the time goes in v1:
time: 752 us; the launch traced here: 750 us
  waiting for transfers between devices  461 us (61%)
  matrix products  143 us (19%)
  local copies, waits for them, and re-layouts  76.8 us (10%)
  starting transfers between devices  48.7 us (6%)
  between operations  14.3 us (2%)
    all_gather x1, waiting for transfers between devices, body(): shard_piece = lax.all_gather(points_map, 'pts', axis=0, tiled=True)  330 us
    all_to_all x1, waiting for transfers between devices, body(): map_full = lax.all_to_all(copies_2, 'pts', 0, 0, tiled=True)  86.7 us
    dot_general x3, matrix products, body(): jnp.einsum('pi,pc->ic', map_full, scaled_cols, preferred_element_type=jnp...  37.8 us
    dot_general x12, matrix products, per_walker(): forward = jnp.dot(left_orb, trial.T, preferred_element_type=jnp.float32)  37.4 us
    dot_general x12, matrix products, per_walker(): jnp.dot(trial_here, right_orb.T, preferred_element_type=jnp.float32)  33.7 us
    all_to_all x3, waiting for transfers between devices, copy_for_each(): return lax.all_to_all(copies, axis, split_axis=0, concat_axis=0, tiled=True)  30.4 us
    all_to_all x3, starting transfers between devices, copy_for_each(): return lax.all_to_all(copies, axis, split_axis=0, concat_axis=0, tiled=True)  30.2 us
    unnamed x49, local copies, waits for them, and re-layouts  30.1 us
  transfers between devices with their start and end apart: 6, of which 5 were waited for; matrix products, arithmetic and copies ran while one was open for 27% of the time, Pallas kernels for 0%

profile of v1, /device:TPU:70, one launch (start us, length us, event | category | flops | bytes accessed | tf_op | source)
XLA Modules:
  0.0 749.8 jit_solution(2324924220041689084)
XLA Ops:
  7.2 3.3 copy.54
  10.5 3.2 convolution_convert_fusion.4
  19.2 17.8 %all-to-all-start.1 = ((bf16[32,200,12]{1,2,0:T(8,128)(2,1)}), bf16[32,200,12]{1,2,0:T(8,128)(2,1)S(1)}, u32[]{:S(2)}, u32[]{:S(2)}) async-start(bf16[32,200,12]{1,2,0:T(8,128)(2,1)} %broadcast_in_dim.50), calls=%async_computation.1 | async-start | bytes 524288 | tf_op jit(solution)/shard_map/all_to_all | solution.py:14
  54.0 5.0 all-to-all-done.1
  62.9 7.4 all-to-all-start.2
  78.1 25.4 %all-to-all-done.2 = f32[32,200,12]{1,2,0:T(8,128)S(1)} async-done(((f32[32,200,12]{1,2,0:T(8,128)}), f32[32,200,12]{1,2,0:T(8,128)S(1)}, u32[]{:S(2)}, u32[]{:S(2)}) %all-to-all-start.2) | async-done | bytes 307232 | tf_op jit(solution)/shard_map/all_to_all | solution.py:14
  104.3 6.1 all-to-all-start
  117.4 329.9 %all-gather.2.cloned.1.call-done = bf16[6400,800]{1,0:T(8,128)(2,1)} async-done(((bf16[200,800]{1,0:T(8,128)(2,1)}), bf16[6400,800]{1,0:T(8,128)(2,1)}) %all-gather.2.cloned.1.call-update) | async-done | bytes 10240016 | tf_op jit(solution)/shard_map/all_gather | solution.py:63
  447.3 28.2 %convolution_convert_fusion = bf16[6400,1536]{0,1:T(8,128)(2,1)} fusion(bf16[6400,800]{1,0:T(8,128)(2,1)} %all-gather.2.cloned.1.call-done, bf16[800,1536]{0,1:T(8,128)(2,1)} %bitcast.67), kind=kOutput, calls=%fused_computation.11 | convolution fusion | flops 15738470400 | bytes 32358400 | tf_op jit(solution)/shard_map/dot_general | solution.py:65
  475.5 26.4 %copy.60 = bf16[6400,12,128]{2,0,1:T(8,128)(2,1)} copy(bf16[6400,12,128]{0,2,1:T(8,128)(2,1)} %bitcast.65) | data formatting | bytes 39321600 | tf_op jit(solution)/shard_map/reshape | solution.py:67
  501.9 81.8 %while.10 = (s32[]{:T(128)}, f32[12]{0:T(128)S(1)}, bf16[12,200,128]{2,1,0:T(8,128)(2,1)}, bf16[6400,128]{1,0:T(8,128)(2,1)S(1)}, f32[200,6400]{1,0:T(8,128)}, /...) while((s32[]{:T(128)}, f32[12]{0:T(128)S(1)}, bf16[12,200,128]{2,1,0:T(8,128)(2,1)}, ...), condition=%wide.region_4.5_spmd, body=%wide.region_2.4_spmd.sunk | while | flops 659200000 | bytes 34100372 | solution.py:77
  504.8 3.1 fusion.62
  511.6 3.1 fusion.62
  518.5 3.1 fusion.62
  525.3 3.1 fusion.62
  532.1 3.1 fusion.62
  538.9 3.1 fusion.62
  583.7 86.7 %all-to-all-done = bf16[32,200,800]{2,1,0:T(8,128)(2,1)} async-done(((bf16[32,200,800]{2,1,0:T(8,128)(2,1)}), bf16[32,200,800]{2,1,0:T(8,128)(2,1)}, u32[]{:S(2)}, u32[]{:S(2)}) %all-to-all-start) | async-done | bytes 10240032 | tf_op jit(solution)/shard_map/all_to_all | solution.py:83
  671.0 4.9 all-to-all-start.4
  675.9 12.6 %convolution_convert_fusion.5 = bf16[800,48]{0,1:T(8,128)(2,1)S(1)} fusion(bf16[6400,800]{1,0:T(8,128)(2,1)} %bitcast.6, f32[48,6400]{1,0:T(8,128)S(1)} %gather_fusion, pred[48]{0:T(512)(128)(4,1)S(1)} %compare_and_fusion, bf16[800,1536]{0,1:T(8,128)(2,1)} %bitcast.68, s32[]{:T(128)S(6)} %select_n.54), kind=kOutput, calls=%fused_computation.33 | convolution fusion | flops 984614400 | bytes 24329268 | tf_op jit(solution)/shard_map/pi,pc->ic/dot_general | solution.py:97
  688.6 12.6 %fusion.17 = bf16[800,48]{0,1:T(8,128)(2,1)S(1)} fusion(bf16[6400,800]{1,0:T(8,128)(2,1)} %bitcast.6, bf16[800,48]{0,1:T(8,128)(2,1)S(1)} %convolution_convert_fusion.5, f32[48,6400]{1,0:T(8,128)S(1)} %gather_fusion, pred[48]{0:T(512)(128)(4,1)S(1)} %compare_and_fusion), kind=kOutput, calls=%fused_computation.28 | convolution fusion | flops 984652800 | bytes 11622448 | tf_op jit(solution)/shard_map/pi,pc->ic/dot_general | solution.py:97
  701.1 12.6 %fusion.21 = bf16[800,48]{0,1:T(8,128)(2,1)S(1)} fusion(bf16[6400,800]{1,0:T(8,128)(2,1)} %bitcast.6, bf16[800,48]{0,1:T(8,128)(2,1)S(1)} %fusion.17, f32[48,6400]{1,0:T(8,128)S(1)} %gather_fusion, pred[48]{0:T(512)(128)(4,1)S(1)} %compare_and_fusion, bf16[800,48]{0,1:T(8,128)(2,1)S(1)} %convolution_convert_fusion.5, bf16[800,1536]{0,1:T(8,128)(2,1)} %bitcast.69, ...), kind=kOutput, calls=%fused_computation.32 | convolution fusion | flops 984960000 | bytes 24587780 | tf_op jit(solution)/shard_map/pi,pc->ic/dot_general | solution.py:97
  715.0 12.2 %all-to-all-start.3 = ((bf16[32,2,600]{2,1,0:T(2,128)(2,1)}), bf16[32,2,600]{2,1,0:T(2,128)(2,1)S(1)}, u32[]{:S(2)}, u32[]{:S(2)}) async-start(bf16[32,2,600]{2,1,0:T(2,128)(2,1)} %reshape.113), calls=%async_computation.3 | async-start | bytes 163840 | tf_op jit(solution)/shard_map/all_to_all | solution.py:102
  727.8 13.8 %all-to-all-done.3 = bf16[32,2,600]{2,1,0:T(2,128)(2,1)S(1)} async-done(((bf16[32,2,600]{2,1,0:T(2,128)(2,1)}), bf16[32,2,600]{2,1,0:T(2,128)(2,1)S(1)}, u32[]{:S(2)}, u32[]{:S(2)}) %all-to-all-start.3) | async-done | bytes 76832 | tf_op jit(solution)/shard_map/all_to_all | solution.py:102
  (168 shorter events, 108.6 us)
Async XLA Ops:
  7.2 29.8 %copy-start = (bf16[200,800]{1,0:T(8,128)(2,1)S(1)}, bf16[200,800]{1,0:T(8,128)(2,1)}, u32[]{:S(2)}) copy-start(bf16[200,800]{1,0:T(8,128)(2,1)} %param.7) | copy-start | bytes 960004
  10.5 43.5 %copy-start.2 = (bf16[800,12,128]{0,2,1:T(8,128)(2,1)}, bf16[800,12,128]{0,2,1:T(8,128)(2,1)S(1)}, u32[]{:S(2)}) copy-start(bf16[800,12,128]{0,2,1:T(8,128)(2,1)S(1)} %copy.54) | copy-start | bytes 7372804
  10.5 49.0 %copy-start.6 = (s32[200,12]{0,1:T(8,128)S(1)}, s32[200,12]{0,1:T(8,128)}, u32[]{:S(2)}) copy-start(s32[200,12]{0,1:T(8,128)} %param.11) | copy-start | bytes 28804
  19.2 39.8 %all-to-all-start.1 = ((bf16[32,200,12]{1,2,0:T(8,128)(2,1)}), bf16[32,200,12]{1,2,0:T(8,128)(2,1)S(1)}, u32[]{:S(2)}, u32[]{:S(2)}) async-start(bf16[32,200,12]{1,2,0:T(8,128)(2,1)} %broadcast_in_dim.50), calls=%async_computation.1 | async-start | bytes 524288 | tf_op jit(solution)/shard_map/all_to_all | solution.py:14
  62.9 40.5 %all-to-all-start.2 = ((f32[32,200,12]{1,2,0:T(8,128)}), f32[32,200,12]{1,2,0:T(8,128)S(1)}, u32[]{:S(2)}, u32[]{:S(2)}) async-start(f32[32,200,12]{1,2,0:T(8,128)} %broadcast_in_dim.51), calls=%async_computation.2 | async-start | bytes 1048576 | tf_op jit(solution)/shard_map/all_to_all | solution.py:14
  104.3 6.9 copy-start.3
  104.3 9.5 %copy-start.4 = (bf16[200,12,128]{2,1,0:T(8,128)(2,1)S(1)}, bf16[200,12,128]{2,1,0:T(8,128)(2,1)}, u32[]{:S(2)}) copy-start(bf16[200,12,128]{2,1,0:T(8,128)(2,1)} %reshape.100) | copy-start | bytes 1843204
  104.3 566.1 %all-to-all-start = ((bf16[32,200,800]{2,1,0:T(8,128)(2,1)}), bf16[32,200,800]{2,1,0:T(8,128)(2,1)}, u32[]{:S(2)}, u32[]{:S(2)}) async-start(bf16[32,200,800]{2,1,0:T(8,128)(2,1)} %bitcast.5), calls=%async_computation | async-start | bytes 22937600 | tf_op jit(solution)/shard_map/all_to_all | solution.py:83
  110.4 336.9 %all-gather.2.cloned.1.call-start = ((), (), s32[]{:S(2)}) async-start(), calls=%async_computation.5 | async-start | bytes 11827200 | tf_op jit(solution)/shard_map/all_gather | solution.py:63
  475.5 26.4 %copy-start.1 = (bf16[6400,128]{1,0:T(8,128)(2,1)S(1)}, bf16[6400,128]{1,0:T(8,128)(2,1)}, u32[]{:S(2)}) copy-start(bf16[6400,128]{1,0:T(8,128)(2,1)} %param.8) | copy-start | bytes 4915204
  501.9 2.9 slice-start.1
  508.7 2.9 slice-start.1
  515.5 2.9 slice-start.1
  522.3 2.9 slice-start.1
  529.1 2.9 slice-start.1
  536.0 2.9 slice-start.1
  542.8 2.9 slice-start.1
  549.6 2.9 slice-start.1
  556.4 2.9 slice-start.1
  563.2 2.9 slice-start.1
  570.0 2.9 slice-start.1
  576.8 2.9 slice-start.1
  671.0 44.0 %all-to-all-start.4 = ((f32[32,1,12]{2,1,0:T(1,128)}), f32[32,1,12]{2,1,0:T(1,128)S(1)}, u32[]{:S(2)}, u32[]{:S(2)}) async-start(f32[32,1,12]{2,1,0:T(1,128)} %broadcast_in_dim.53), calls=%async_computation.4 | async-start | bytes 32768 | tf_op jit(solution)/shard_map/all_to_all | solution.py:14
  715.0 26.6 %all-to-all-start.3 = ((bf16[32,2,600]{2,1,0:T(2,128)(2,1)}), bf16[32,2,600]{2,1,0:T(2,128)(2,1)S(1)}, u32[]{:S(2)}, u32[]{:S(2)}) async-start(bf16[32,2,600]{2,1,0:T(2,128)(2,1)} %reshape.113), calls=%async_computation.3 | async-start | bytes 163840 | tf_op jit(solution)/shard_map/all_to_all | solution.py:102
  (13 other events, 34.6 us)
Sparse Core Ops, SparseCore 0:
  112.9 334.2 all-gather.1
